TPU v7x, 8 devices: a whole 2x2x1 slice. The times are simulated.
8 devices in a mesh: data: 2 (over z, y), tp: 4 (over x, core).
Axes of the slice: x: 2, y: 2, z: 1, core: 2. Of those that a mesh axis runs over, the one named last changes fastest.
Arguments:
- x_in: bfloat16 [8192, 5120], P('data'), parts along dimension 0
- w_gate: bfloat16 [5120, 13824], P(None, 'tp')
- w_up: bfloat16 [5120, 13824], P(None, 'tp')
- w_down: bfloat16 [13824, 5120], P('tp')
- residual: bfloat16 [8192, 5120], P(('data', 'tp')), parts along dimension 0
- norm_gain: float32 [5120], replicated
Outputs:
- output 1: bfloat16 [8192, 5120], P(('data', 'tp')), parts along dimension 0
- output 2: bfloat16 [8192, 5120], P(('data', 'tp')), parts along dimension 0
There are 2 independent parts. A program takes and returns all parts, laid end to end along the dimension named above; an argument that names none is the same for every part.
All inputs are finite; a program needn't handle non-finite values.
Results may differ from a plain program's by a relative error of at most 0.00659832.
Values are sent between devices in bfloat16 or wider.
A program may use at most 1 GiB of HBM per device.

v0:
```python
import jax
import jax.numpy as jnp
from jax import lax
from jax.sharding import PartitionSpec as P

EPS = 1e-5


def add_and_norm(y_sum, residual, norm_gain):
    hidden_sum = residual.astype(jnp.float32) + y_sum
    mean_sq = jnp.mean(hidden_sum * hidden_sum, axis=-1, keepdims=True)
    normed = hidden_sum * lax.rsqrt(mean_sq + EPS) * norm_gain
    return hidden_sum.astype(jnp.bfloat16), normed.astype(jnp.bfloat16)


def solution(mesh):
    tp_size = mesh.shape["tp"]

    def local_block(x_in, w_gate, w_up, w_down, residual, norm_gain):
        gate_val = jnp.dot(x_in, w_gate, preferred_element_type=jnp.float32)
        up_val = jnp.dot(x_in, w_up, preferred_element_type=jnp.float32)
        hidden = (jax.nn.silu(gate_val) * up_val).astype(jnp.bfloat16)
        part_prod = jnp.dot(hidden, w_down, preferred_element_type=jnp.float32).astype(jnp.bfloat16)
        received = lax.all_to_all(part_prod, "tp", 0, 0, tiled=True)
        rows = residual.shape[0]
        y_sum = jnp.sum(received.reshape(tp_size, rows, received.shape[1]), axis=0, dtype=jnp.float32)
        return add_and_norm(y_sum, residual, norm_gain)

    row_spec = P(("data", "tp"), None)
    return jax.shard_map(local_block, mesh=mesh, in_specs=(P("data", None), P(None, "tp"), P(None, "tp"), P("tp", None), row_spec, P(None)), out_specs=(row_spec, row_spec), check_vma=False)
```

profile of v0, /device:TPU:0, one launch (start us, length us, event | category | flops | bytes accessed | tf_op | source)
XLA Modules:
  0.0 1017.4 jit_solution(11776331343908952996)
XLA Ops:
  0.6 163.7 %fusion.1 = f32[4096,3456]{1,0:T(8,128)} fusion(bf16[4096,5120]{1,0:T(8,128)(2,1)} %param.6, bf16[5120,3456]{1,0:T(8,128)(2,1)} %param.7), kind=kOutput, calls=%fused_computation.8 | convolution fusion | flops 144955146240 | bytes 133955584 | tf_op jit(solution)/shard_map/dot_general | solution.py:20
  164.3 170.3 %multiply_convert_fusion = bf16[4096,3456]{1,0:T(8,128)(2,1)} fusion(f32[4096,3456]{1,0:T(8,128)} %fusion.1, bf16[4096,5120]{1,0:T(8,128)(2,1)} %param.6, bf16[5120,3456]{1,0:T(8,128)(2,1)} %param.8), kind=kOutput, calls=%fused_computation.1 | convolution fusion | flops 145040080896 | bytes 162267136 | tf_op jit(solution)/shard_map/dot_general | solution.py:21
  334.6 163.7 %convolution_convert_fusion = bf16[4096,5120]{1,0:T(8,128)(2,1)} fusion(bf16[4096,3456]{1,0:T(8,128)(2,1)} %multiply_convert_fusion, bf16[3456,5120]{1,0:T(8,128)(2,1)} %param.9), kind=kOutput, calls=%fused_computation.2 | convolution fusion | flops 144976117760 | bytes 105644032 | tf_op jit(solution)/shard_map/dot_general | solution.py:23
  498.3 475.4 %all_to_all.9 = bf16[4,1024,5120]{2,1,0:T(8,128)(2,1)} all-to-all(bf16[4,1024,5120]{2,1,0:T(8,128)(2,1)} %bitcast.7), channel_id=1, replica_groups=mesh['data'=2,'tp'=4] {'tp'}, dimensions={0} | all-to-all | bytes 83886080 | tf_op jit(solution)/shard_map/all_to_all | solution.py:24
  973.7 0.0 copy-start
  973.7 24.2 %convert_reduce_fusion = f32[1024,5120]{1,0:T(8,128)S(1)} fusion(bf16[4,1024,5120]{2,1,0:T(8,128)(2,1)} %all_to_all.9), kind=kLoop, calls=%fused_computation | loop fusion | flops 36700160 | bytes 62914560 | tf_op jit(solution)/shard_map/reduce_sum | solution.py:26
  997.9 6.8 multiply_reduce_fusion
  1004.7 0.0 copy-done
  1004.7 12.7 %multiply_convert_fusion.1 = (bf16[1024,5120]{1,0:T(8,128)(2,1)}, bf16[1024,5120]{1,0:T(8,128)(2,1)}) fusion(f32[5120]{0:T(1024)S(1)} %copy-done, f32[1024]{0:T(1024)S(1)} %add_rsqrt_fusion, f32[1024,5120]{1,0:T(8,128)S(1)} %convert_reduce_fusion, bf16[1024,5120]{1,0:T(8,128)(2,1)} %param.10), kind=kLoop, calls=%fused_computation.3 | loop fusion | flops 31457280 | bytes 52453376 | tf_op jit(solution)/shard_map/convert_element_type | solution.py:13
  (1 shorter events, 0.0 us)
Async XLA Ops:
  973.7 31.0 %copy-start = (f32[5120]{0:T(1024)S(1)}, f32[5120]{0:T(1024)}, u32[]{:S(2)}) copy-start(f32[5120]{0:T(1024)} %param.11) | copy-start | bytes 61444
where the time goes:
time: 1020 us
  matrix products  498 us (49%)
  blocking collectives  475 us (47%)
  other arithmetic  43.7 us (4%)
    all_to_all x1, blocking collectives, local_block(): received = lax.all_to_all(part_prod, 'tp', 0, 0, tiled=True)  475 us
    dot_general x1, matrix products, local_block(): up_val = jnp.dot(x_in, w_up, preferred_element_type=jnp.float32)  170 us
    dot_general x1, matrix products, local_block(): jnp.dot(hidden, w_down, preferred_element_type=jnp.float32)  164 us
    dot_general x1, matrix products, local_block(): gate_val = jnp.dot(x_in, w_gate, preferred_element_type=jnp.float32)  164 us
    reduce_sum x1, other arithmetic, local_block(): jnp.sum(received.reshape(tp_size, rows, received.shape[1]), axis=0, dtype...  24.2 us

commit v1 on v0

v1 whole, which is shorter than its diff:
```python
import functools

import jax
import jax.numpy as jnp
from jax import lax
from jax.experimental import pallas as pl
from jax.experimental.pallas import tpu as pltpu
from jax.sharding import PartitionSpec as P

EPS = 1e-5
TF = 384
TD = 512
HALVES = (192, 320, 512)
VMEM = 67043328
MESH = pl.DeviceIdType.MESH


def block_kernel(nf, nd, block, x_hbm, w_gate, w_up, w_down, residual, h_out, recv, stage, x, gate_buf, up_buf, down_buf, hidden, y_buf, in_buf, res_buf, h_buf, x_sem, gate_sem, up_sem, down_sem, stage_sem, send_sem, recv_sem, in_sem, res_sem, h_sem):
    me = lax.axis_index("tp")
    partner = me + 1 - 2 * lax.rem(me, 2)
    far = (lax.rem(me + 2, 4), lax.rem(partner + 2, 4))

    chunks = []
    at = 0
    for half in HALVES:
        chunks.append([(far[0], 0, at, half), (far[1], 1, at, half)])
        at += half
    chunks.append([(partner, 2, 0, block)])
    chunks.append([(me, 3, 0, block)])
    n_chunks = len(chunks)

    def x_copies(k):
        copies, row = [], 0
        for i, (owner, _, first, size) in enumerate(chunks[k]):
            src = x_hbm.at[pl.ds(pl.multiple_of(owner * block + first, 64), size)]
            copies.append(pltpu.make_async_copy(src, x.at[pl.ds(row, size)], x_sem.at[i]))
            row += size
        return copies

    def gate_copies(tile, slot):
        cols = pl.ds(pl.multiple_of(tile * TF, 128), TF)
        return [
            pltpu.make_async_copy(w_gate.at[:, cols], gate_buf.at[slot], gate_sem.at[slot]),
            pltpu.make_async_copy(w_up.at[:, cols], up_buf.at[slot], up_sem.at[slot]),
        ]

    def down_copy(tile, slot):
        cols = pl.ds(pl.multiple_of(tile * TD, 128), TD)
        return pltpu.make_async_copy(w_down.at[:, cols], down_buf.at[slot], down_sem.at[slot])

    def stage_copies(k, tile, slot):
        copies, row = [], 0
        for i, (_, src, first, size) in enumerate(chunks[k]):
            copies.append(pltpu.make_async_copy(y_buf.at[slot, pl.ds(row, size)], stage.at[tile, src, pl.ds(first, size)], stage_sem.at[slot, i]))
            row += size
        return copies

    def send_copies(k, tile):
        return [
            pltpu.make_async_remote_copy(
                src_ref=stage.at[tile, src, pl.ds(first, size)],
                dst_ref=recv.at[tile, src, pl.ds(first, size)],
                send_sem=send_sem,
                recv_sem=recv_sem.at[tile],
                device_id={"tp": owner},
                device_id_type=MESH,
            )
            for owner, src, first, size in chunks[k]
        ]

    def flush(k, tile, slot):
        for copy in stage_copies(k, tile, slot):
            copy.wait()
        for copy in send_copies(k, tile):
            copy.start()

    def in_copies(tile, slot):
        cols = pl.ds(pl.multiple_of(tile * TD, 128), TD)
        return [
            pltpu.make_async_copy(recv.at[tile], in_buf.at[slot], in_sem.at[slot]),
            pltpu.make_async_copy(residual.at[:, cols], res_buf.at[slot], res_sem.at[slot]),
        ]

    def h_copy(tile, slot):
        cols = pl.ds(pl.multiple_of(tile * TD, 128), TD)
        return pltpu.make_async_copy(h_buf.at[slot], h_out.at[:, cols], h_sem.at[slot])

    def fetch_in(tile, slot):
        pltpu.make_async_copy(recv.at[tile], recv.at[tile], recv_sem.at[tile]).wait()
        for copy in in_copies(tile, slot):
            copy.start()

    for copy in (*gate_copies(0, 0), *x_copies(0), *gate_copies(1, 1), down_copy(0, 0), down_copy(1, 1)):
        copy.start()
    barrier = pltpu.get_barrier_semaphore()
    for peer in (partner, *far):
        pl.semaphore_signal(barrier, inc=1, device_id={"tp": peer}, device_id_type=MESH)
    pl.semaphore_wait(barrier, 3)

    for k in range(n_chunks):
        rows = sum(size for _, _, _, size in chunks[k])
        last = k == n_chunks - 1
        for copy in x_copies(k):
            copy.wait()

        def gate_step(i, _, k=k, rows=rows):
            slot = lax.rem(k * nf + i, 2)
            for copy in gate_copies(i, slot):
                copy.wait()
            for piece in range(TF // 128):
                cols = slice(piece * 128, piece * 128 + 128)
                both = jnp.concatenate([gate_buf[slot, :, cols], up_buf[slot, :, cols]], axis=1)
                prod = jnp.dot(x[0:rows, :], both, preferred_element_type=jnp.float32)
                val = (jax.nn.silu(prod[:, :128]) * prod[:, 128:]).astype(jnp.bfloat16)
                hidden[0:rows, pl.ds(pl.multiple_of(i * TF + piece * 128, 128), 128)] = val
            if k == n_chunks - 1:

                @pl.when(i + 2 < nf)
                def _():
                    for copy in gate_copies(i + 2, slot):
                        copy.start()
            else:
                for copy in gate_copies(lax.rem(i + 2, nf), slot):
                    copy.start()
            return 0

        lax.fori_loop(0, nf, gate_step, 0)
        if k > 0:
            flush(k - 1, nd - 1, (nd - 1) % 2)
        if not last:
            for copy in x_copies(k + 1):
                copy.start()
        else:
            fetch_in(0, 0)

        def down_step(j, _, k=k, rows=rows, last=last):
            slot = lax.rem(j, 2)
            down_copy(j, slot).wait()
            prod = jnp.dot(hidden[0:rows, :], down_buf[slot], preferred_element_type=jnp.float32).astype(jnp.bfloat16)
            if not last:
                y_buf[slot, 0:rows] = prod

                @pl.when(j > 0)
                def _():
                    flush(k, j - 1, 1 - slot)

                for copy in stage_copies(k, j, slot):
                    copy.start()
                down_copy(lax.rem(j + 2, nd), slot).start()
            else:
                for copy in in_copies(j, slot):
                    copy.wait()

                @pl.when(j >= 2)
                def _():
                    h_copy(j - 2, slot).wait()

                total = prod.astype(jnp.float32) + in_buf[slot, 0].astype(jnp.float32)
                total = total + in_buf[slot, 1].astype(jnp.float32) + in_buf[slot, 2].astype(jnp.float32)
                h_buf[slot] = res_buf[slot].astype(jnp.float32) + total
                h_copy(j, slot).start()

                @pl.when(j + 2 < nd)
                def _():
                    down_copy(j + 2, slot).start()

                @pl.when(j + 1 < nd)
                def _():
                    fetch_in(j + 1, 1 - slot)

            return 0

        lax.fori_loop(0, nd, down_step, 0)

    for tile in (nd - 2, nd - 1):
        h_copy(tile, tile % 2).wait()
    pltpu.make_async_copy(stage, stage, send_sem).wait()


def block_sum(x_in, w_gate, w_up, w_down, residual):
    d_model, d_hidden = w_gate.shape
    block = residual.shape[0]
    rows = block
    nf, nd = d_hidden // TF, d_model // TD
    any_spec = pl.BlockSpec(memory_space=pl.ANY)
    bf16, f32 = jnp.bfloat16, jnp.float32
    dma = pltpu.SemaphoreType.DMA
    return pl.pallas_call(
        functools.partial(block_kernel, nf, nd, block),
        in_specs=[any_spec] * 5,
        out_specs=[any_spec] * 3,
        out_shape=[
            jax.ShapeDtypeStruct((block, d_model), f32),
            jax.ShapeDtypeStruct((nd, 3, block, TD), bf16),
            jax.ShapeDtypeStruct((nd, 3, block, TD), bf16),
        ],
        scratch_shapes=[
            pltpu.VMEM((rows, d_model), bf16),
            pltpu.VMEM((2, d_model, TF), bf16),
            pltpu.VMEM((2, d_model, TF), bf16),
            pltpu.VMEM((2, d_hidden, TD), bf16),
            pltpu.VMEM((rows, d_hidden), bf16),
            pltpu.VMEM((2, rows, TD), bf16),
            pltpu.VMEM((2, 3, block, TD), bf16),
            pltpu.VMEM((2, block, TD), bf16),
            pltpu.VMEM((2, block, TD), f32),
            dma((2,)),
            dma((2,)),
            dma((2,)),
            dma((2,)),
            dma((2, 2)),
            dma,
            dma((nd,)),
            dma((2,)),
            dma((2,)),
            dma((2,)),
        ],
        compiler_params=pltpu.CompilerParams(vmem_limit_bytes=VMEM, collective_id=0, has_side_effects=True),
        cost_estimate=pl.CostEstimate(flops=24 * block * d_model * d_hidden, bytes_accessed=36 * d_model * d_hidden, transcendentals=0),
        name="block_sum",
    )(x_in, w_gate, w_up, w_down, residual)[0]


def norm_kernel(h_ref, gain, h_out, n_out):
    h = h_ref[...]
    mean_sq = jnp.mean(h * h, axis=-1, keepdims=True)
    h_out[...] = h.astype(jnp.bfloat16)
    n_out[...] = (h * lax.rsqrt(mean_sq + EPS) * gain[...]).astype(jnp.bfloat16)


def norm_rows(h, gain):
    block, d_model = h.shape
    rows = 128
    spec = pl.BlockSpec((rows, d_model), lambda i: (i, 0))
    out = jax.ShapeDtypeStruct(h.shape, jnp.bfloat16)
    return pl.pallas_call(
        norm_kernel,
        grid=(block // rows,),
        in_specs=[spec, pl.BlockSpec((1, d_model), lambda i: (0, 0))],
        out_specs=[spec, spec],
        out_shape=[out, out],
        cost_estimate=pl.CostEstimate(flops=5 * block * d_model, bytes_accessed=8 * block * d_model, transcendentals=block),
        name="norm_rows",
    )(h, gain)


def solution(mesh):
    def local_block(x_in, w_gate, w_up, w_down, residual, norm_gain):
        h = block_sum(x_in, w_gate, w_up, w_down, residual)
        return tuple(norm_rows(h, norm_gain.reshape(1, -1)))

    row_spec = P(("data", "tp"), None)
    return jax.shard_map(local_block, mesh=mesh, in_specs=(P("data", None), P(None, "tp"), P(None, "tp"), P("tp", None), row_spec, P(None)), out_specs=(row_spec, row_spec), check_vma=False)
```

time: 1020 us -> 514 us (0.50)
  Pallas kernels: 0 us -> 513 us
  matrix products: 498 us -> 0 us
  blocking collectives: 475 us -> 0 us
  other arithmetic: 43.7 us -> 0 us
    pallas_call x0 -> x2, Pallas kernels: none -> 513 us  [the longest x1 497 us: block_sum(): pl.pallas_call(functools.partial(block_kernel, nf, nd, block), in_specs=[...]
    dot_general x3 -> x0, matrix products: 498 us -> none  [the longest x1 170 us: local_block(): up_val = jnp.dot(x_in, w_up, preferred_element_type=jnp.float32)]
    all_to_all x1 -> x0, blocking collectives: 475 us -> none  [local_block(): received = lax.all_to_all(part_prod, 'tp', 0, 0, tiled=True)]
    reduce_sum x2 -> x0, other arithmetic: 31 us -> none  [the longest x1 24.2 us: local_block(): jnp.sum(received.reshape(tp_size, rows, received.shape[1]), axis=0, dtype...]
    convert_element_type x1 -> x0, other arithmetic: 12.7 us -> none  [add_and_norm(): return (hidden_sum.astype(jnp.bfloat16), normed.astype(jnp.bfloat16))]
where the time goes in v1:
time: 514 us
  Pallas kernels  513 us (100%)
    pallas_call x1, Pallas kernels, block_sum(): pl.pallas_call(functools.partial(block_kernel, nf, nd, block), in_specs=[...  497 us
    pallas_call x1, Pallas kernels, norm_rows(): pl.pallas_call(norm_kernel, grid=(block // rows,), in_specs=[spec, pl.Blo...  16.5 us

profile of v1, /device:TPU:0, one launch (start us, length us, event | category | flops | bytes accessed | tf_op | source)
XLA Modules:
  0.0 513.7 jit_solution(5298562460229767095)
XLA Ops:
  0.6 496.6 %block_sum.1 = (f32[1024,5120]{1,0:T(8,128)}, bf16[10,3,1024,512]{3,2,1,0:T(8,128)(2,1)}, bf16[10,3,1024,512]{3,2,1,0:T(8,128)(2,1)}) custom-call(bf16[4096,5120]{1,0:T(8,128)(2,1)} %x_hbm.1, bf16[5120,3456]{1,0:T(8,128)(2,1)} %w_gate.1, bf16[5120,3456]{1,0:T(8,128)(2,1)} %w_up.1, bf16[3456,5120]{1,0:T(8,128)(2,1)} %w_down.1, bf16[1024,5120]{1,0:T(8,128)(2,1)} %residual.1), custom_call_target="tpu_custom_call" | custom-call | flops 434865438720 | bytes 637009920 | tf_op jit(solution)/shard_map/block_sum/pallas_call | solution.py:188
  497.2 16.5 %norm_rows.1 = (bf16[1024,5120]{1,0:T(8,128)(2,1)}, bf16[1024,5120]{1,0:T(8,128)(2,1)}) custom-call(f32[1024,5120]{1,0:T(8,128)} %get-tuple-element.3.h_ref, f32[1,5120]{1,0:T(1,128)} %bitcast.1), custom_call_target="tpu_custom_call" | custom-call | flops 26214400 | bytes 41943040 | tf_op jit(solution)/shard_map/norm_rows/pallas_call | solution.py:236

commit v2 on v1

--- a/solution.py
+++ b/solution.py
@@ -10,12 +10,12 @@
 EPS = 1e-5
 TF = 384
 TD = 512
-HALVES = (192, 320, 512)
+HALVES = (160, 320, 544)
 VMEM = 67043328
 MESH = pl.DeviceIdType.MESH
 
 
-def block_kernel(nf, nd, block, x_hbm, w_gate, w_up, w_down, residual, h_out, recv, stage, x, gate_buf, up_buf, down_buf, hidden, y_buf, in_buf, res_buf, h_buf, x_sem, gate_sem, up_sem, down_sem, stage_sem, send_sem, recv_sem, in_sem, res_sem, h_sem):
+def block_kernel(nf, nd, block, x_hbm, w_gate, w_up, w_down, residual, h_out, sq_out, recv, stage, x, gate_buf, up_buf, down_buf, hidden, y_buf, in_buf, res_buf, h_buf, sq_buf, x_sem, gate_sem, up_sem, down_sem, stage_sem, send_sem, recv_sem, in_sem, res_sem, h_sem, sq_sem):
     me = lax.axis_index("tp")
     partner = me + 1 - 2 * lax.rem(me, 2)
     far = (lax.rem(me + 2, 4), lax.rem(partner + 2, 4))
@@ -32,7 +32,7 @@
     def x_copies(k):
         copies, row = [], 0
         for i, (owner, _, first, size) in enumerate(chunks[k]):
-            src = x_hbm.at[pl.ds(pl.multiple_of(owner * block + first, 64), size)]
+            src = x_hbm.at[pl.ds(pl.multiple_of(owner * block + first, 32), size)]
             copies.append(pltpu.make_async_copy(src, x.at[pl.ds(row, size)], x_sem.at[i]))
             row += size
         return copies
@@ -90,7 +90,7 @@
         for copy in in_copies(tile, slot):
             copy.start()
 
-    for copy in (*gate_copies(0, 0), *x_copies(0), *gate_copies(1, 1), down_copy(0, 0), down_copy(1, 1)):
+    for copy in (*x_copies(0), *gate_copies(0, 0), *gate_copies(1, 1)):
         copy.start()
     barrier = pltpu.get_barrier_semaphore()
     for peer in (partner, *far):
@@ -124,7 +124,13 @@
                     copy.start()
             return 0
 
-        lax.fori_loop(0, nf, gate_step, 0)
+        if k == 0:
+            lax.fori_loop(0, nf - 3, gate_step, 0)
+            for tile in (0, 1):
+                down_copy(tile, tile).start()
+            lax.fori_loop(nf - 3, nf, gate_step, 0)
+        else:
+            lax.fori_loop(0, nf, gate_step, 0)
         if k > 0:
             flush(k - 1, nd - 1, (nd - 1) % 2)
         if not last:
@@ -133,54 +139,84 @@
         else:
             fetch_in(0, 0)
 
-        def down_step(j, _, k=k, rows=rows, last=last):
+        if last:
+            break
+
+        def down_step(j, _, k=k, rows=rows):
             slot = lax.rem(j, 2)
             down_copy(j, slot).wait()
-            prod = jnp.dot(hidden[0:rows, :], down_buf[slot], preferred_element_type=jnp.float32).astype(jnp.bfloat16)
-            if not last:
-                y_buf[slot, 0:rows] = prod
-
-                @pl.when(j > 0)
-                def _():
-                    flush(k, j - 1, 1 - slot)
-
-                for copy in stage_copies(k, j, slot):
-                    copy.start()
-                down_copy(lax.rem(j + 2, nd), slot).start()
-            else:
-                for copy in in_copies(j, slot):
-                    copy.wait()
-
-                @pl.when(j >= 2)
-                def _():
-                    h_copy(j - 2, slot).wait()
-
-                total = prod.astype(jnp.float32) + in_buf[slot, 0].astype(jnp.float32)
-                total = total + in_buf[slot, 1].astype(jnp.float32) + in_buf[slot, 2].astype(jnp.float32)
-                h_buf[slot] = res_buf[slot].astype(jnp.float32) + total
-                h_copy(j, slot).start()
-
-                @pl.when(j + 2 < nd)
-                def _():
-                    down_copy(j + 2, slot).start()
-
-                @pl.when(j + 1 < nd)
-                def _():
-                    fetch_in(j + 1, 1 - slot)
-
+            y_buf[slot, 0:rows] = jnp.dot(hidden[0:rows, :], down_buf[slot], preferred_element_type=jnp.float32).astype(jnp.bfloat16)
+
+            @pl.when(j > 0)
+            def _():
+                flush(k, j - 1, 1 - slot)
+
+            for copy in stage_copies(k, j, slot):
+                copy.start()
+            down_copy(lax.rem(j + 2, nd), slot).start()
             return 0
 
         lax.fori_loop(0, nd, down_step, 0)
 
-    for tile in (nd - 2, nd - 1):
-        h_copy(tile, tile % 2).wait()
+    def own_dot(slot):
+        y_buf[slot, 0:block] = jnp.dot(hidden[0:block, :], down_buf[slot], preferred_element_type=jnp.float32).astype(jnp.bfloat16)
+
+    def combine(slot):
+        total = y_buf[slot, 0:block].astype(jnp.float32) + in_buf[slot, 2].astype(jnp.float32)
+        total = total + in_buf[slot, 0].astype(jnp.float32) + in_buf[slot, 1].astype(jnp.float32)
+        h = res_buf[slot].astype(jnp.float32) + total
+        h_buf[slot] = h
+        sq = h * h
+        acc = sq_buf[...]
+        for c in range(TD // 128):
+            acc = acc + sq[:, c * 128 : c * 128 + 128]
+        sq_buf[...] = acc
+
+    sq_buf[...] = jnp.zeros_like(sq_buf)
+    down_copy(0, 0).wait()
+    own_dot(0)
+    down_copy(2, 0).start()
+
+    def own_step(j, _):
+        slot = lax.rem(j, 2)
+        down_copy(j, slot).wait()
+        for copy in in_copies(j - 1, 1 - slot):
+            copy.wait()
+
+        @pl.when(j >= 3)
+        def _():
+            h_copy(j - 3, 1 - slot).wait()
+
+        combine(1 - slot)
+        own_dot(slot)
+        h_copy(j - 1, 1 - slot).start()
+
+        @pl.when(j + 2 < nd)
+        def _():
+            down_copy(j + 2, slot).start()
+
+        fetch_in(j, slot)
+        return 0
+
+    lax.fori_loop(1, nd, own_step, 0)
+    end = (nd - 1) % 2
+    for copy in in_copies(nd - 1, end):
+        copy.wait()
+    h_copy(nd - 3, end).wait()
+    combine(end)
+    h_copy(nd - 1, end).start()
+    sq_copy = pltpu.make_async_copy(sq_buf, sq_out, sq_sem)
+    sq_copy.start()
+    h_copy(nd - 2, 1 - end).wait()
+    h_copy(nd - 1, end).wait()
+    sq_copy.wait()
     pltpu.make_async_copy(stage, stage, send_sem).wait()
 
 
 def block_sum(x_in, w_gate, w_up, w_down, residual):
     d_model, d_hidden = w_gate.shape
     block = residual.shape[0]
-    rows = block
+    rows = max(block, 2 * max(HALVES))
     nf, nd = d_hidden // TF, d_model // TD
     any_spec = pl.BlockSpec(memory_space=pl.ANY)
     bf16, f32 = jnp.bfloat16, jnp.float32
@@ -188,9 +224,10 @@
     return pl.pallas_call(
         functools.partial(block_kernel, nf, nd, block),
         in_specs=[any_spec] * 5,
-        out_specs=[any_spec] * 3,
+        out_specs=[any_spec] * 4,
         out_shape=[
             jax.ShapeDtypeStruct((block, d_model), f32),
+            jax.ShapeDtypeStruct((block, 128), f32),
             jax.ShapeDtypeStruct((nd, 3, block, TD), bf16),
             jax.ShapeDtypeStruct((nd, 3, block, TD), bf16),
         ],
@@ -204,6 +241,7 @@
             pltpu.VMEM((2, 3, block, TD), bf16),
             pltpu.VMEM((2, block, TD), bf16),
             pltpu.VMEM((2, block, TD), f32),
+            pltpu.VMEM((block, 128), f32),
             dma((2,)),
             dma((2,)),
             dma((2,)),
@@ -214,21 +252,23 @@
             dma((2,)),
             dma((2,)),
             dma((2,)),
+            dma,
         ],
         compiler_params=pltpu.CompilerParams(vmem_limit_bytes=VMEM, collective_id=0, has_side_effects=True),
         cost_estimate=pl.CostEstimate(flops=24 * block * d_model * d_hidden, bytes_accessed=36 * d_model * d_hidden, transcendentals=0),
         name="block_sum",
-    )(x_in, w_gate, w_up, w_down, residual)[0]
-
-
-def norm_kernel(h_ref, gain, h_out, n_out):
+    )(x_in, w_gate, w_up, w_down, residual)[:2]
+
+
+def norm_kernel(h_ref, sq, gain, h_out, n_out):
+    d_model = h_ref.shape[1]
     h = h_ref[...]
-    mean_sq = jnp.mean(h * h, axis=-1, keepdims=True)
+    scale = lax.rsqrt(jnp.sum(sq[...], axis=1, keepdims=True) / d_model + EPS)
     h_out[...] = h.astype(jnp.bfloat16)
-    n_out[...] = (h * lax.rsqrt(mean_sq + EPS) * gain[...]).astype(jnp.bfloat16)
-
-
-def norm_rows(h, gain):
+    n_out[...] = (h * scale * gain[...]).astype(jnp.bfloat16)
+
+
+def norm_rows(h, sq, gain):
     block, d_model = h.shape
     rows = 128
     spec = pl.BlockSpec((rows, d_model), lambda i: (i, 0))
@@ -236,18 +276,18 @@
     return pl.pallas_call(
         norm_kernel,
         grid=(block // rows,),
-        in_specs=[spec, pl.BlockSpec((1, d_model), lambda i: (0, 0))],
+        in_specs=[spec, pl.BlockSpec((rows, 128), lambda i: (i, 0)), pl.BlockSpec((1, d_model), lambda i: (0, 0))],
         out_specs=[spec, spec],
         out_shape=[out, out],
         cost_estimate=pl.CostEstimate(flops=5 * block * d_model, bytes_accessed=8 * block * d_model, transcendentals=block),
         name="norm_rows",
-    )(h, gain)
+    )(h, sq, gain)
 
 
 def solution(mesh):
     def local_block(x_in, w_gate, w_up, w_down, residual, norm_gain):
-        h = block_sum(x_in, w_gate, w_up, w_down, residual)
-        return tuple(norm_rows(h, norm_gain.reshape(1, -1)))
+        h, sq = block_sum(x_in, w_gate, w_up, w_down, residual)
+        return tuple(norm_rows(h, sq, norm_gain.reshape(1, -1)))
 
     row_spec = P(("data", "tp"), None)
     return jax.shard_map(local_block, mesh=mesh, in_specs=(P("data", None), P(None, "tp"), P(None, "tp"), P("tp", None), row_spec, P(None)), out_specs=(row_spec, row_spec), check_vma=False)

time: 514 us -> 532 us (1.035)
  Pallas kernels: 513 us -> 531 us
    pallas_call x1, Pallas kernels: 497 us -> 515 us  [block_sum(): pl.pallas_call(functools.partial(block_kernel, nf, nd, block), in_specs=[...]
where the time goes in v2:
time: 532 us
  Pallas kernels  531 us (100%)
    pallas_call x1, Pallas kernels, block_sum(): pl.pallas_call(functools.partial(block_kernel, nf, nd, block), in_specs=[...  515 us
    pallas_call x1, Pallas kernels, norm_rows(): pl.pallas_call(norm_kernel, grid=(block // rows,), in_specs=[spec, pl.Blo...  16.4 us

profile of v2, /device:TPU:0, one launch (start us, length us, event | category | flops | bytes accessed | tf_op | source)
XLA Modules:
  0.0 531.8 jit_solution(4411732302230192051)
XLA Ops:
  0.6 514.8 %block_sum.1 = (f32[1024,5120]{1,0:T(8,128)}, f32[1024,128]{1,0:T(8,128)}, bf16[10,3,1024,512]{3,2,1,0:T(8,128)(2,1)}, bf16[10,3,1024,512]{3,2,1,0:T(8,128)(2,1)}) custom-call(bf16[4096,5120]{1,0:T(8,128)(2,1)} %x_hbm.1, bf16[5120,3456]{1,0:T(8,128)(2,1)} %w_gate.1, bf16[5120,3456]{1,0:T(8,128)(2,1)} %w_up.1, bf16[3456,5120]{1,0:T(8,128)(2,1)} %w_down.1, ...), custom_call_target="tpu_custom_call" | custom-call | flops 434865438720 | bytes 637009920 | tf_op jit(solution)/shard_map/block_sum/pallas_call | solution.py:224
  515.4 16.4 %norm_rows.1 = (bf16[1024,5120]{1,0:T(8,128)(2,1)}, bf16[1024,5120]{1,0:T(8,128)(2,1)}) custom-call(f32[1024,5120]{1,0:T(8,128)} %get-tuple-element.4.h_ref, f32[1024,128]{1,0:T(8,128)} %get-tuple-element.5.sq, f32[1,5120]{1,0:T(1,128)} %bitcast.1), custom_call_target="tpu_custom_call" | custom-call | flops 26214400 | bytes 41943040 | tf_op jit(solution)/shard_map/norm_rows/pallas_call | solution.py:276

commit v3 on v2

--- a/solution.py
+++ b/solution.py
@@ -10,7 +10,7 @@
 EPS = 1e-5
 TF = 384
 TD = 512
-HALVES = (160, 320, 544)
+HALVES = (160, 352, 512)
 VMEM = 67043328
 MESH = pl.DeviceIdType.MESH
 
@@ -113,6 +113,18 @@
                 prod = jnp.dot(x[0:rows, :], both, preferred_element_type=jnp.float32)
                 val = (jax.nn.silu(prod[:, :128]) * prod[:, 128:]).astype(jnp.bfloat16)
                 hidden[0:rows, pl.ds(pl.multiple_of(i * TF + piece * 128, 128), 128)] = val
+            if k == 0:
+
+                @pl.when(i == nf - 4)
+                def _():
+                    for tile in (0, 1):
+                        down_copy(tile, tile).start()
+            else:
+
+                @pl.when(i == 0)
+                def _():
+                    flush(k - 1, nd - 1, (nd - 1) % 2)
+
             if k == n_chunks - 1:
 
                 @pl.when(i + 2 < nf)
@@ -124,15 +136,7 @@
                     copy.start()
             return 0
 
-        if k == 0:
-            lax.fori_loop(0, nf - 3, gate_step, 0)
-            for tile in (0, 1):
-                down_copy(tile, tile).start()
-            lax.fori_loop(nf - 3, nf, gate_step, 0)
-        else:
-            lax.fori_loop(0, nf, gate_step, 0)
-        if k > 0:
-            flush(k - 1, nd - 1, (nd - 1) % 2)
+        lax.fori_loop(0, nf, gate_step, 0)
         if not last:
             for copy in x_copies(k + 1):
                 copy.start()

time: 532 us -> 531 us (level)
  no operation moved by 1% of the time
where the time goes in v3:
time: 531 us
  Pallas kernels  530 us (100%)
    pallas_call x1, Pallas kernels, block_sum(): pl.pallas_call(functools.partial(block_kernel, nf, nd, block), in_specs=[...  514 us
    pallas_call x1, Pallas kernels, norm_rows(): pl.pallas_call(norm_kernel, grid=(block // rows,), in_specs=[spec, pl.Blo...  16.4 us

profile of v3, /device:TPU:0, one launch (start us, length us, event | category | flops | bytes accessed | tf_op | source)
XLA Modules:
  0.0 530.9 jit_solution(730260353220920550)
XLA Ops:
  0.6 513.8 %block_sum.1 = (f32[1024,5120]{1,0:T(8,128)}, f32[1024,128]{1,0:T(8,128)}, bf16[10,3,1024,512]{3,2,1,0:T(8,128)(2,1)}, bf16[10,3,1024,512]{3,2,1,0:T(8,128)(2,1)}) custom-call(bf16[4096,5120]{1,0:T(8,128)(2,1)} %x_hbm.1, bf16[5120,3456]{1,0:T(8,128)(2,1)} %w_gate.1, bf16[5120,3456]{1,0:T(8,128)(2,1)} %w_up.1, bf16[3456,5120]{1,0:T(8,128)(2,1)} %w_down.1, ...), custom_call_target="tpu_custom_call" | custom-call | flops 434865438720 | bytes 637009920 | tf_op jit(solution)/shard_map/block_sum/pallas_call | solution.py:228
  514.5 16.4 %norm_rows.1 = (bf16[1024,5120]{1,0:T(8,128)(2,1)}, bf16[1024,5120]{1,0:T(8,128)(2,1)}) custom-call(f32[1024,5120]{1,0:T(8,128)} %get-tuple-element.4.h_ref, f32[1024,128]{1,0:T(8,128)} %get-tuple-element.5.sq, f32[1,5120]{1,0:T(1,128)} %bitcast.1), custom_call_target="tpu_custom_call" | custom-call | flops 26214400 | bytes 41943040 | tf_op jit(solution)/shard_map/norm_rows/pallas_call | solution.py:280

commit v4 on v3

--- a/solution.py
+++ b/solution.py
@@ -180,6 +180,7 @@
     down_copy(0, 0).wait()
     own_dot(0)
     down_copy(2, 0).start()
+    fetch_in(1, 1)
 
     def own_step(j, _):
         slot = lax.rem(j, 2)
@@ -199,11 +200,15 @@
         def _():
             down_copy(j + 2, slot).start()
 
-        fetch_in(j, slot)
+        @pl.when(j + 2 < nd)
+        def _():
+            fetch_in(j + 1, 1 - slot)
+
         return 0
 
     lax.fori_loop(1, nd, own_step, 0)
     end = (nd - 1) % 2
+    fetch_in(nd - 1, end)
     for copy in in_copies(nd - 1, end):
         copy.wait()
     h_copy(nd - 3, end).wait()

time: 531 us -> 514 us (0.968)
  Pallas kernels: 530 us -> 513 us
    pallas_call x1, Pallas kernels: 514 us -> 496 us  [block_sum(): pl.pallas_call(functools.partial(block_kernel, nf, nd, block), in_specs=[...]
where the time goes in v4:
time: 514 us; the launch traced here: 513 us
  Pallas kernels  513 us (100%)
    pallas_call x1, Pallas kernels, block_sum(): pl.pallas_call(functools.partial(block_kernel, nf, nd, block), in_specs=[...  496 us
    pallas_call x1, Pallas kernels, norm_rows(): pl.pallas_call(norm_kernel, grid=(block // rows,), in_specs=[spec, pl.Blo...  16.4 us

profile of v4, /device:TPU:0, one launch (start us, length us, event | category | flops | bytes accessed | tf_op | source)
XLA Modules:
  0.0 513.2 jit_solution(9745484558005511877)
XLA Ops:
  0.6 496.2 %block_sum.1 = (f32[1024,5120]{1,0:T(8,128)}, f32[1024,128]{1,0:T(8,128)}, bf16[10,3,1024,512]{3,2,1,0:T(8,128)(2,1)}, bf16[10,3,1024,512]{3,2,1,0:T(8,128)(2,1)}) custom-call(bf16[4096,5120]{1,0:T(8,128)(2,1)} %x_hbm.1, bf16[5120,3456]{1,0:T(8,128)(2,1)} %w_gate.1, bf16[5120,3456]{1,0:T(8,128)(2,1)} %w_up.1, bf16[3456,5120]{1,0:T(8,128)(2,1)} %w_down.1, ...), custom_call_target="tpu_custom_call" | custom-call | flops 434865438720 | bytes 637009920 | tf_op jit(solution)/shard_map/block_sum/pallas_call | solution.py:233
  496.8 16.4 %norm_rows.1 = (bf16[1024,5120]{1,0:T(8,128)(2,1)}, bf16[1024,5120]{1,0:T(8,128)(2,1)}) custom-call(f32[1024,5120]{1,0:T(8,128)} %get-tuple-element.4.h_ref, f32[1024,128]{1,0:T(8,128)} %get-tuple-element.5.sq, f32[1,5120]{1,0:T(1,128)} %bitcast.1), custom_call_target="tpu_custom_call" | custom-call | flops 26214400 | bytes 41943040 | tf_op jit(solution)/shard_map/norm_rows/pallas_call | solution.py:285

commit v5 on v4

--- a/solution.py
+++ b/solution.py
@@ -10,7 +10,7 @@
 EPS = 1e-5
 TF = 384
 TD = 512
-HALVES = (160, 352, 512)
+HALVES = (192, 320, 512)
 VMEM = 67043328
 MESH = pl.DeviceIdType.MESH
 
@@ -39,10 +39,13 @@
 
     def gate_copies(tile, slot):
         cols = pl.ds(pl.multiple_of(tile * TF, 128), TF)
-        return [
-            pltpu.make_async_copy(w_gate.at[:, cols], gate_buf.at[slot], gate_sem.at[slot]),
-            pltpu.make_async_copy(w_up.at[:, cols], up_buf.at[slot], up_sem.at[slot]),
-        ]
+        half = w_gate.shape[0] // 2
+        copies = []
+        for part in range(2):
+            here = pl.ds(part * half, half)
+            copies.append(pltpu.make_async_copy(w_gate.at[here, cols], gate_buf.at[slot, here], gate_sem.at[slot, part]))
+            copies.append(pltpu.make_async_copy(w_up.at[here, cols], up_buf.at[slot, here], up_sem.at[slot, part]))
+        return copies
 
     def down_copy(tile, slot):
         cols = pl.ds(pl.multiple_of(tile * TD, 128), TD)
@@ -252,8 +255,8 @@
             pltpu.VMEM((2, block, TD), f32),
             pltpu.VMEM((block, 128), f32),
             dma((2,)),
-            dma((2,)),
-            dma((2,)),
+            dma((2, 2)),
+            dma((2, 2)),
             dma((2,)),
             dma((2, 2)),
             dma,

time: 514 us -> 514 us (level)
  no operation moved by 1% of the time
where the time goes in v5:
time: 514 us; the launch traced here: 513 us
  Pallas kernels  513 us (100%)
    pallas_call x1, Pallas kernels, block_sum(): pl.pallas_call(functools.partial(block_kernel, nf, nd, block), in_specs=[...  496 us
    pallas_call x1, Pallas kernels, norm_rows(): pl.pallas_call(norm_kernel, grid=(block // rows,), in_specs=[spec, pl.Blo...  16.4 us

profile of v5, /device:TPU:0, one launch (start us, length us, event | category | flops | bytes accessed | tf_op | source)
XLA Modules:
  0.0 513.3 jit_solution(15977408869079790970)
XLA Ops:
  0.6 496.2 %block_sum.1 = (f32[1024,5120]{1,0:T(8,128)}, f32[1024,128]{1,0:T(8,128)}, bf16[10,3,1024,512]{3,2,1,0:T(8,128)(2,1)}, bf16[10,3,1024,512]{3,2,1,0:T(8,128)(2,1)}) custom-call(bf16[4096,5120]{1,0:T(8,128)(2,1)} %x_hbm.1, bf16[5120,3456]{1,0:T(8,128)(2,1)} %w_gate.1, bf16[5120,3456]{1,0:T(8,128)(2,1)} %w_up.1, bf16[3456,5120]{1,0:T(8,128)(2,1)} %w_down.1, ...), custom_call_target="tpu_custom_call" | custom-call | flops 434865438720 | bytes 637009920 | tf_op jit(solution)/shard_map/block_sum/pallas_call | solution.py:236
  496.9 16.4 %norm_rows.1 = (bf16[1024,5120]{1,0:T(8,128)(2,1)}, bf16[1024,5120]{1,0:T(8,128)(2,1)}) custom-call(f32[1024,5120]{1,0:T(8,128)} %get-tuple-element.4.h_ref, f32[1024,128]{1,0:T(8,128)} %get-tuple-element.5.sq, f32[1,5120]{1,0:T(1,128)} %bitcast.1), custom_call_target="tpu_custom_call" | custom-call | flops 26214400 | bytes 41943040 | tf_op jit(solution)/shard_map/norm_rows/pallas_call | solution.py:288
